TPU v7x, 256 devices: a whole 4x4x8 slice. The times are simulated.
256 devices in a mesh: panel: 32 (over y, x, core), samp: 8 (over z).
Axes of the slice: x: 4, y: 4, z: 8, core: 2. Of those that a mesh axis runs over, the one named last changes fastest.
Arguments:
- called_allele_tallies: int32 [4096, 1024], P('samp'), may hold values from 0 to 2
- presence_flags: int32 [4096, 1024], P('samp'), may hold values 0 or 1
- reference_panel_strands: int32 [65536, 1024], P('panel'), may hold values from 0 to 1
- softmax_sharpness: float32 [4096], P('samp'), may hold values from 0.02 to 4
- trait_measurements: float32 [4096], P('samp'), may hold values from -8 to 8
- cohort_membership: int32 [4096], P('samp'), may hold values from 0 to 7, as said below
Outputs:
- dosage_out: bfloat16 [4096, 1024], P('samp', 'panel')
- zscore: float32 [1024], P('panel')
Inputs may be any that keep to these rules, and one draw needn't show every extreme that they name: `cohort_membership`: every group id from 0 to 7 occurs.
All inputs are finite; a program needn't handle non-finite values. No bound on the sum of `presence_flags` on one device may be relied on, other than what follows from the above.
Results may differ from a plain program's by a relative error of at most 0.0055.
Values sent between devices are 32-bit elements; how exact they have to be, the bound alone decides.
No kernel may reach another device: no remote copies, remote signals or barrier semaphores. Data moves between devices by JAX's collectives and lax.ppermute only.
A program may use at most 64 MiB of HBM per device.

v0:
```python
import jax
import jax.numpy as jnp
from jax import lax
from jax.sharding import Mesh
from jax.sharding import PartitionSpec as P

GROUPS = 8
PANEL = ("panel_0", "panel_1", "panel_2")
log_two = 0.6931471805599453


def copy_for_each(shard, axis):
    count = lax.axis_size(axis)
    return lax.all_to_all(
        jnp.broadcast_to(shard[None], (count, *shard.shape)), axis, 0, 0, tiled=True
    )


def of_everyone(shard, axis):
    return copy_for_each(shard, axis).sum(axis=0)


def over_copies(shard, axis):
    return copy_for_each(shard, axis).max(axis=0)


def over_axes(shard, axes):
    for axis in axes:
        shard = lax.psum(shard, axis)
    return shard


def in_blocks(shard, dim, count):
    before, after = (shard.shape[:dim], shard.shape[dim + 1 :])
    return jnp.moveaxis(shard.reshape(*before, count, -1, *after), dim, 0)


def sent_and_summed(shard, axis, dim):
    count = lax.axis_size(axis)
    pieces = lax.all_to_all(in_blocks(shard, dim, count), axis, 0, 0, tiled=True)
    return jnp.sum(pieces, axis=0)


def together(arrays, axis):
    line, at, gathered = (jnp.concatenate([a.reshape(-1) for a in arrays]), 0, [])
    so_far = of_everyone(line, axis)
    for a in arrays:
        gathered.append(so_far[at : at + a.size].reshape(a.shape))
        at += a.size
    return tuple(gathered)


def on_device(
    called_allele_tallies,
    presence_flags,
    reference_panel_strands,
    softmax_sharpness,
    trait_measurements,
    cohort_membership,
):
    panel_count = lax.axis_size(PANEL)
    sample_rows, variants = called_allele_tallies.shape
    local_haps = reference_panel_strands.shape[0]
    hap_float = reference_panel_strands.astype(jnp.float32)
    allele_counts = of_everyone(jnp.sum(hap_float, axis=0), PANEL)
    allele_freq = allele_counts / float(local_haps * panel_count)
    geno_float = called_allele_tallies.astype(jnp.float32)
    observed_f = presence_flags.astype(jnp.float32)
    demeaned_expected_count = (observed_f * (geno_float - 2.0 * allele_freq[None, :])).astype(
        jnp.bfloat16
    )
    tile_first_entry = jnp.sum(
        demeaned_expected_count.astype(jnp.float32) * allele_freq[None, :], axis=1
    )
    hap_bf = reference_panel_strands.astype(jnp.bfloat16)
    raw_efficient_statistic = lax.dot_general(
        demeaned_expected_count,
        hap_bf,
        (((1,), (1,)), ((), ())),
        preferred_element_type=jnp.float32,
    )
    panel_match_energies = softmax_sharpness[:, None] * (
        raw_efficient_statistic - tile_first_entry[:, None]
    )
    local_steps = jnp.ceil(jnp.max(panel_match_energies, axis=1) / log_two)
    share = variants // panel_count
    first_column = lax.axis_index(PANEL) * share
    peak_steps = over_copies(local_steps, PANEL)
    weights = jnp.exp(panel_match_energies - log_two * peak_steps[:, None])
    weight_total = over_axes(jnp.sum(weights, axis=1), PANEL)
    partial_dose = 2.0 * jnp.dot(
        weights.astype(jnp.bfloat16), hap_bf, preferred_element_type=jnp.float32
    )
    own_dose = sent_and_summed(partial_dose, PANEL, 1)
    expected_allele_count = own_dose / weight_total[:, None]
    own_geno = lax.dynamic_slice_in_dim(geno_float, first_column, share, 1)
    own_observed = lax.dynamic_slice_in_dim(presence_flags, first_column, share, 1)
    dosage = jnp.where(own_observed == 1, own_geno, expected_allele_count)
    dosage_out = dosage.astype(jnp.bfloat16)
    member = (cohort_membership[:, None] == jnp.arange(GROUPS, dtype=jnp.int32)[None, :]).astype(
        jnp.float32
    )
    group_sum_local = jnp.dot(trait_measurements, member, precision=lax.Precision.HIGHEST)
    group_count_local = jnp.sum(member, axis=0)
    dose_sum_local = jnp.sum(dosage, axis=0)
    dose_square_local = jnp.sum(dosage * dosage, axis=0)
    all_samples = float(sample_rows * lax.axis_size("samp"))
    local_cross = jnp.dot(trait_measurements, dosage, precision=lax.Precision.HIGHEST)
    local_group_dose = jnp.dot(member.T, dosage, precision=lax.Precision.HIGHEST)
    cross, group_dose, dose_sum, dose_square, group_sum, group_count, pheno_square = together(
        (
            local_cross,
            local_group_dose,
            dose_sum_local,
            dose_square_local,
            group_sum_local,
            group_count_local,
            jnp.sum(trait_measurements * trait_measurements),
        ),
        "samp",
    )
    group_mean = group_sum / group_count
    score_u = cross - jnp.dot(group_mean, group_dose, precision=lax.Precision.HIGHEST)
    resid_square = pheno_square - jnp.sum(group_sum * group_mean)
    sigma = resid_square / (all_samples - GROUPS)
    dose_mean = dose_sum / all_samples
    spread = dose_square / all_samples - dose_mean * dose_mean
    zscore = score_u / jnp.sqrt(sigma * all_samples * (spread + 1e-05))
    return (dosage_out, zscore)


def solution(mesh):
    finer = Mesh(
        mesh.devices.reshape(4, 4, 2, mesh.shape["samp"]), ("panel_0", "panel_1", "panel_2", "samp")
    )
    placed = (P("samp", None), P("samp", None), P(PANEL, None), P("samp"), P("samp"), P("samp"))
    return jax.shard_map(
        on_device,
        mesh=finer,
        in_specs=placed,
        out_specs=(P("samp", PANEL), P(PANEL)),
        check_vma=False,
    )
```

profile of v0, /device:TPU:1, one launch (start us, length us, event | category | flops | bytes accessed | tf_op | source)
XLA Modules:
  0.0 123.2 jit_solution(13171496174605333055)
XLA Ops:
  0.6 4.2 %convert_reduce_fusion = f32[1024]{0:T(1024)S(1)} fusion(s32[2048,1024]{1,0:T(8,128)} %param.8), kind=kLoop, calls=%fused_computation | loop fusion | flops 4193280 | bytes 8392704 | tf_op jit(solution)/shard_map/reduce_sum | solution.py:65
  4.8 0.7 broadcast_in_dim.6
  5.5 8.6 %all-to-all-start = ((f32[32,1,1024]{2,1,0:T(1,128)}), f32[32,1,1024]{2,1,0:T(1,128)S(1)}, u32[]{:S(2)}, u32[]{:S(2)}) async-start(f32[32,1,1024]{2,1,0:T(1,128)} %broadcast_in_dim.6), calls=%async_computation | async-start | bytes 262144 | tf_op jit(solution)/shard_map/all_to_all | solution.py:14
  14.1 1.9 %copy.19 = s32[512,1024]{0,1:T(8,128)} copy(s32[512,1024]{1,0:T(8,128)S(1)} %copy-done) | data formatting | bytes 4194304 | tf_op args[1]
  16.0 1.9 %copy.20 = s32[512,1024]{0,1:T(8,128)S(1)} copy(s32[512,1024]{1,0:T(8,128)} %param.6) | data formatting | bytes 4194304 | tf_op args[0]
  17.9 3.8 %all-to-all-done = f32[32,1,1024]{2,1,0:T(1,128)S(1)} async-done(((f32[32,1,1024]{2,1,0:T(1,128)}), f32[32,1,1024]{2,1,0:T(1,128)S(1)}, u32[]{:S(2)}, u32[]{:S(2)}) %all-to-all-start) | async-done | bytes 131104 | tf_op jit(solution)/shard_map/all_to_all | solution.py:14
  21.8 2.1 %multiply_reduce_fusion = (f32[512]{0:T(512)S(1)}, bf16[512,1024]{0,1:T(8,128)(2,1)S(1)}) fusion(f32[1024]{0:T(1024)S(1)} %get-tuple-element.8, f32[1024]{0:T(1024)S(1)} %get-tuple-element.7, s32[512,1024]{0,1:T(8,128)S(1)} %copy.20, s32[512,1024]{0,1:T(8,128)} %copy.19), kind=kLoop, calls=%fused_computation.9 | loop fusion | flops 4193792 | bytes 5253120 | tf_op jit(solution)/shard_map/reduce_sum | solution.py:72
  23.9 7.9 %fusion = (f32[512]{0:T(512)S(1)}, f32[512,2048]{1,0:T(8,128)}) fusion(f32[512]{0:T(512)S(1)} %get-tuple-element.5, f32[512]{0:T(512)S(1)} %copy-done.3, bf16[512,1024]{0,1:T(8,128)(2,1)S(1)} %get-tuple-element.6, s32[2048,1024]{1,0:T(8,128)} %param.8), kind=kOutput, calls=%fused_computation.3 | convolution fusion | flops 2152726016 | bytes 13637632 | tf_op jit(solution)/shard_map/dot_general | solution.py:76
  31.9 11.0 %all_to_all.23 = f32[32,1,512]{2,1,0:T(1,128)S(1)} all-to-all(f32[32,1,512]{2,1,0:T(1,128)S(1)} %broadcast_in_dim.7), channel_id=1, replica_groups=mesh['panel_0'=4,'panel_1'=4,'panel_2'=2,'samp'=8] {'panel_0','panel_1',..., dimensions={0} | all-to-all | bytes 131072 | tf_op jit(solution)/shard_map/all_to_all | solution.py:14
  42.9 8.5 %fusion.11 = f32[512,1024]{1,0:T(8,128)} fusion(s32[2048,1024]{1,0:T(8,128)} %param.8, f32[512,2048]{1,0:T(8,128)} %get-tuple-element.10, f32[512]{0:T(512)S(1)} %broadcast_multiply_fusion.2, f32[512]{0:T(512)S(1)} %get-tuple-element.5, f32[512]{0:T(512)S(1)} %copy-done.3), kind=kOutput, calls=%fused_computation.15 | convolution fusion | flops 2154299392 | bytes 14686208 | tf_op jit(solution)/shard_map/dot_general | solution.py:91
  51.4 2.9 %copy.24 = f32[512,1024]{0,1:T(8,128)} copy(f32[512,1024]{1,0:T(8,128)} %fusion.11) | data formatting | bytes 4194304 | tf_op jit(solution)/shard_map/mul | solution.py:91
  54.3 4.9 %all-to-all-start.2 = ((f32[32,512,32]{1,2,0:T(8,128)}), f32[32,512,32]{1,2,0:T(8,128)}, u32[]{:S(2)}, u32[]{:S(2)}) async-start(f32[32,512,32]{1,2,0:T(8,128)} %bitcast.26), calls=%async_computation.2 | async-start | bytes 4194304 | tf_op jit(solution)/shard_map/all_to_all | solution.py:40
  59.2 1.6 %convert_element_type.27 = f32[512,1024]{0,1:T(8,128)} convert(s32[512,1024]{0,1:T(8,128)S(1)} %copy.20) | non-fusion elementwise | flops 524288 | bytes 4194304 | tf_op jit(solution)/shard_map/convert_element_type | solution.py:67
  60.8 0.6 multiply_reduce_fusion.2
  61.4 0.1 convert_reduce_fusion.1
  61.5 0.1 convolution_bitcast_fusion
  61.7 3.2 %fusion.1 = f32[512]{0:T(512)S(1)} fusion(f32[512,2048]{1,0:T(8,128)} %get-tuple-element.10, f32[512]{0:T(512)S(1)} %broadcast_multiply_fusion.2, f32[512]{0:T(512)S(1)} %get-tuple-element.5, f32[512]{0:T(512)S(1)} %copy-done.3), kind=kLoop, calls=%fused_computation.4 | loop fusion | flops 4193792 | bytes 4202496 | tf_op jit(solution)/shard_map/reduce_sum | solution.py:90
  64.8 19.8 %psum.21 = f32[512]{0:T(512)S(1)} all-reduce(f32[512]{0:T(512)S(1)} %fusion.1), channel_id=1, replica_groups=mesh['panel_0'=4,'panel_1'=4,'panel_2'=2,'samp'=8] {'panel_0'}, use_global_device_ids=true, to_apply=%region_7.0 | all-reduce | flops 512 | bytes 4096 | tf_op jit(solution)/shard_map/psum | solution.py:29
  84.7 8.9 %psum.22 = f32[512]{0:T(512)S(1)} all-reduce(f32[512]{0:T(512)S(1)} %psum.21), channel_id=1, replica_groups=mesh['panel_0'=4,'panel_1'=4,'panel_2'=2,'samp'=8] {'panel_1'}, use_global_device_ids=true, to_apply=%region_8.0 | all-reduce | flops 512 | bytes 4096 | tf_op jit(solution)/shard_map/psum | solution.py:29
  93.5 6.8 %psum.23 = f32[512]{0:T(512)S(1)} all-reduce(f32[512]{0:T(512)S(1)} %psum.22), channel_id=1, replica_groups=mesh['panel_0'=4,'panel_1'=4,'panel_2'=2,'samp'=8] {'panel_2'}, use_global_device_ids=true, to_apply=%region_9.0 | all-reduce | flops 512 | bytes 4096 | tf_op jit(solution)/shard_map/psum | solution.py:29
  100.3 1.7 %reduce_sum.102 = f32[512,32]{0,1:T(8,128)S(1)} reduce(f32[32,512,32]{1,2,0:T(8,128)} %all-to-all-done.2, f32[]{:T(128)} %constant.45.clone.1), dimensions={0}, to_apply=%region_5.0 | reduce | flops 507904 | bytes 2162692 | tf_op jit(solution)/shard_map/reduce_sum | solution.py:41
  102.0 1.0 multiply_reduce_fusion.1
  103.0 0.1 fusion.18
  103.2 0.2 convolution_bitcast_fusion.1
  103.4 0.8 concatenate.3
  104.2 0.6 broadcast_in_dim.8
  104.8 8.2 %all-to-all-start.3 = ((f32[8,1,369]{2,1,0:T(1,128)}), f32[8,1,369]{2,1,0:T(1,128)S(1)}, u32[]{:S(2)}, u32[]{:S(2)}) async-start(f32[8,1,369]{2,1,0:T(1,128)} %broadcast_in_dim.8), calls=%async_computation.3 | async-start | bytes 24576 | tf_op jit(solution)/shard_map/all_to_all | solution.py:14
  113.0 0.6 convert_element_type.34
  113.6 6.0 %all-to-all-done.3 = f32[8,1,369]{2,1,0:T(1,128)S(1)} async-done(((f32[8,1,369]{2,1,0:T(1,128)}), f32[8,1,369]{2,1,0:T(1,128)S(1)}, u32[]{:S(2)}, u32[]{:S(2)}) %all-to-all-start.3) | async-done | bytes 11840 | tf_op jit(solution)/shard_map/all_to_all | solution.py:14
  119.6 0.6 slice.25
  120.2 0.8 multiply_reduce_fusion.3
  122.4 0.7 fusion.17
  (19 shorter events, 0.5 us)
Async XLA Ops:
  0.6 13.5 %copy-start = (s32[512,1024]{1,0:T(8,128)S(1)}, s32[512,1024]{1,0:T(8,128)}, u32[]{:S(2)}) copy-start(s32[512,1024]{1,0:T(8,128)} %param.7) | copy-start | bytes 6291460
  5.5 16.2 %all-to-all-start = ((f32[32,1,1024]{2,1,0:T(1,128)}), f32[32,1,1024]{2,1,0:T(1,128)S(1)}, u32[]{:S(2)}, u32[]{:S(2)}) async-start(f32[32,1,1024]{2,1,0:T(1,128)} %broadcast_in_dim.6), calls=%async_computation | async-start | bytes 262144 | tf_op jit(solution)/shard_map/all_to_all | solution.py:14
  16.0 8.0 %copy-start.3 = (f32[512]{0:T(512)S(1)}, f32[512]{0:T(512)}, u32[]{:S(2)}) copy-start(f32[512]{0:T(512)} %param.9) | copy-start | bytes 6148
  54.3 6.5 %copy-start.2 = (f32[512]{0:T(512)S(1)}, f32[512]{0:T(512)}, u32[]{:S(2)}) copy-start(f32[512]{0:T(512)} %param.10) | copy-start | bytes 6148
  54.3 7.1 %copy-start.1 = (s32[512]{0:T(512)S(1)}, s32[512]{0:T(512)}, u32[]{:S(2)}) copy-start(s32[512]{0:T(512)} %param.11) | copy-start | bytes 6148
  54.3 46.0 %all-to-all-start.2 = ((f32[32,512,32]{1,2,0:T(8,128)}), f32[32,512,32]{1,2,0:T(8,128)}, u32[]{:S(2)}, u32[]{:S(2)}) async-start(f32[32,512,32]{1,2,0:T(8,128)} %bitcast.26), calls=%async_computation.2 | async-start | bytes 4194304 | tf_op jit(solution)/shard_map/all_to_all | solution.py:40
  104.8 14.8 %all-to-all-start.3 = ((f32[8,1,369]{2,1,0:T(1,128)}), f32[8,1,369]{2,1,0:T(1,128)S(1)}, u32[]{:S(2)}, u32[]{:S(2)}) async-start(f32[8,1,369]{2,1,0:T(1,128)} %broadcast_in_dim.8), calls=%async_computation.3 | async-start | bytes 24576 | tf_op jit(solution)/shard_map/all_to_all | solution.py:14
where the time goes:
time: 124 us; the launch traced here: 123 us
  blocking collectives  46.4 us (37%)
  starting transfers between devices  21.6 us (17%)
  matrix products  17.5 us (14%)
  other arithmetic  16.1 us (13%)
  waiting for transfers between devices  9.77 us (8%)
  local copies, waits for them, and re-layouts  9.63 us (8%)
  between operations  2.06 us (2%)
    psum x3, blocking collectives, over_axes(): shard = lax.psum(shard, axis)  35.4 us
    all_to_all x2, starting transfers between devices, copy_for_each(): lax.all_to_all(jnp.broadcast_to(shard[None], (count, *shard.shape)), axis...  16.8 us
    all_to_all x1, blocking collectives, copy_for_each(): lax.all_to_all(jnp.broadcast_to(shard[None], (count, *shard.shape)), axis...  11 us
    all_to_all x2, waiting for transfers between devices, copy_for_each(): lax.all_to_all(jnp.broadcast_to(shard[None], (count, *shard.shape)), axis...  9.77 us
    dot_general x1, matrix products, on_device(): jnp.dot(weights.astype(jnp.bfloat16), hap_bf, preferred_element_type=jnp....  8.51 us
    dot_general x1, matrix products, on_device(): lax.dot_general(demeaned_expected_count, hap_bf, (((1,), (1,)), ((), ()))...  7.89 us
    all_to_all x1, starting transfers between devices, sent_and_summed(): lax.all_to_all(in_blocks(shard, dim, count), axis, 0, 0, tiled=True)  4.86 us
    reduce_sum x1, other arithmetic, on_device(): allele_counts = of_everyone(jnp.sum(hap_float, axis=0), PANEL)  4.17 us
  transfers between devices with their start and end apart: 3, of which 2 were waited for; matrix products, arithmetic and copies ran while one was open for 8% of the time, Pallas kernels for 0%

commit v1 on v0

--- a/solution.py
+++ b/solution.py
@@ -26,7 +26,7 @@
 
 def over_axes(shard, axes):
     for axis in axes:
-        shard = lax.psum(shard, axis)
+        shard = jnp.sum(lax.all_gather(shard, axis), axis=0)
     return shard
 
 

time: 124 us -> 127 us (1.024)
  blocking collectives: 46.4 us -> 49.5 us
    all_gather x0 -> x3, blocking collectives: none -> 38.5 us  [over_axes(): shard = jnp.sum(lax.all_gather(shard, axis), axis=0)]
    psum x3 -> x0, blocking collectives: 35.4 us -> none  [over_axes(): shard = lax.psum(shard, axis)]
where the time goes in v1:
time: 127 us; the launch traced here: 126 us
  blocking collectives  49.5 us (39%)
  starting transfers between devices  21.6 us (17%)
  matrix products  17.5 us (14%)
  other arithmetic  16.2 us (13%)
  waiting for transfers between devices  9.77 us (8%)
  local copies, waits for them, and re-layouts  9.63 us (8%)
  between operations  2.06 us (2%)
    all_gather x3, blocking collectives, over_axes(): shard = jnp.sum(lax.all_gather(shard, axis), axis=0)  38.5 us
    all_to_all x2, starting transfers between devices, copy_for_each(): lax.all_to_all(jnp.broadcast_to(shard[None], (count, *shard.shape)), axis...  16.8 us
    all_to_all x1, blocking collectives, copy_for_each(): lax.all_to_all(jnp.broadcast_to(shard[None], (count, *shard.shape)), axis...  11 us
    all_to_all x2, waiting for transfers between devices, copy_for_each(): lax.all_to_all(jnp.broadcast_to(shard[None], (count, *shard.shape)), axis...  9.77 us
    dot_general x1, matrix products, on_device(): jnp.dot(weights.astype(jnp.bfloat16), hap_bf, preferred_element_type=jnp....  8.51 us
    dot_general x1, matrix products, on_device(): lax.dot_general(demeaned_expected_count, hap_bf, (((1,), (1,)), ((), ()))...  7.89 us
    all_to_all x1, starting transfers between devices, sent_and_summed(): lax.all_to_all(in_blocks(shard, dim, count), axis, 0, 0, tiled=True)  4.86 us
    reduce_sum x1, other arithmetic, on_device(): allele_counts = of_everyone(jnp.sum(hap_float, axis=0), PANEL)  4.17 us
  transfers between devices with their start and end apart: 3, of which 2 were waited for; matrix products, arithmetic and copies ran while one was open for 8% of the time, Pallas kernels for 0%

profile of v1, /device:TPU:1, one launch (start us, length us, event | category | flops | bytes accessed | tf_op | source)
XLA Modules:
  0.0 126.3 jit_solution(2019284538045139443)
XLA Ops:
  0.6 4.2 %convert_reduce_fusion = f32[1024]{0:T(1024)S(1)} fusion(s32[2048,1024]{1,0:T(8,128)} %param.8), kind=kLoop, calls=%fused_computation | loop fusion | flops 4193280 | bytes 8392704 | tf_op jit(solution)/shard_map/reduce_sum | solution.py:65
  4.8 0.7 broadcast_in_dim.6
  5.5 8.6 %all-to-all-start = ((f32[32,1,1024]{2,1,0:T(1,128)}), f32[32,1,1024]{2,1,0:T(1,128)S(1)}, u32[]{:S(2)}, u32[]{:S(2)}) async-start(f32[32,1,1024]{2,1,0:T(1,128)} %broadcast_in_dim.6), calls=%async_computation | async-start | bytes 262144 | tf_op jit(solution)/shard_map/all_to_all | solution.py:14
  14.1 1.9 %copy.23 = s32[512,1024]{0,1:T(8,128)} copy(s32[512,1024]{1,0:T(8,128)S(1)} %copy-done) | data formatting | bytes 4194304 | tf_op args[1]
  16.0 1.9 %copy.24 = s32[512,1024]{0,1:T(8,128)S(1)} copy(s32[512,1024]{1,0:T(8,128)} %param.6) | data formatting | bytes 4194304 | tf_op args[0]
  17.9 3.8 %all-to-all-done = f32[32,1,1024]{2,1,0:T(1,128)S(1)} async-done(((f32[32,1,1024]{2,1,0:T(1,128)}), f32[32,1,1024]{2,1,0:T(1,128)S(1)}, u32[]{:S(2)}, u32[]{:S(2)}) %all-to-all-start) | async-done | bytes 131104 | tf_op jit(solution)/shard_map/all_to_all | solution.py:14
  21.8 2.1 %multiply_reduce_fusion = (f32[512]{0:T(512)S(1)}, bf16[512,1024]{0,1:T(8,128)(2,1)S(1)}) fusion(f32[1024]{0:T(1024)S(1)} %get-tuple-element.8, f32[1024]{0:T(1024)S(1)} %get-tuple-element.7, s32[512,1024]{0,1:T(8,128)S(1)} %copy.24, s32[512,1024]{0,1:T(8,128)} %copy.23), kind=kLoop, calls=%fused_computation.9 | loop fusion | flops 4193792 | bytes 5253120 | tf_op jit(solution)/shard_map/reduce_sum | solution.py:72
  23.9 7.9 %fusion = (f32[512]{0:T(512)S(1)}, f32[512,2048]{1,0:T(8,128)}) fusion(f32[512]{0:T(512)S(1)} %get-tuple-element.5, f32[512]{0:T(512)S(1)} %copy-done.3, bf16[512,1024]{0,1:T(8,128)(2,1)S(1)} %get-tuple-element.6, s32[2048,1024]{1,0:T(8,128)} %param.8), kind=kOutput, calls=%fused_computation.3 | convolution fusion | flops 2152726016 | bytes 13637632 | tf_op jit(solution)/shard_map/dot_general | solution.py:76
  31.9 11.0 %all_to_all.23 = f32[32,1,512]{2,1,0:T(1,128)S(1)} all-to-all(f32[32,1,512]{2,1,0:T(1,128)S(1)} %broadcast_in_dim.7), channel_id=1, replica_groups=mesh['panel_0'=4,'panel_1'=4,'panel_2'=2,'samp'=8] {'panel_0','panel_1',..., dimensions={0} | all-to-all | bytes 131072 | tf_op jit(solution)/shard_map/all_to_all | solution.py:14
  42.9 8.5 %fusion.11 = f32[512,1024]{1,0:T(8,128)} fusion(s32[2048,1024]{1,0:T(8,128)} %param.8, f32[512,2048]{1,0:T(8,128)} %get-tuple-element.10, f32[512]{0:T(512)S(1)} %broadcast_multiply_fusion.2, f32[512]{0:T(512)S(1)} %get-tuple-element.5, f32[512]{0:T(512)S(1)} %copy-done.3), kind=kOutput, calls=%fused_computation.15 | convolution fusion | flops 2154299392 | bytes 14686208 | tf_op jit(solution)/shard_map/dot_general | solution.py:91
  51.4 2.9 %copy.28 = f32[512,1024]{0,1:T(8,128)} copy(f32[512,1024]{1,0:T(8,128)} %fusion.11) | data formatting | bytes 4194304 | tf_op jit(solution)/shard_map/mul | solution.py:91
  54.3 4.9 %all-to-all-start.2 = ((f32[32,512,32]{1,2,0:T(8,128)}), f32[32,512,32]{1,2,0:T(8,128)}, u32[]{:S(2)}, u32[]{:S(2)}) async-start(f32[32,512,32]{1,2,0:T(8,128)} %bitcast.29), calls=%async_computation.2 | async-start | bytes 4194304 | tf_op jit(solution)/shard_map/all_to_all | solution.py:40
  59.2 1.6 %convert_element_type.27 = f32[512,1024]{0,1:T(8,128)} convert(s32[512,1024]{0,1:T(8,128)S(1)} %copy.24) | non-fusion elementwise | flops 524288 | bytes 4194304 | tf_op jit(solution)/shard_map/convert_element_type | solution.py:67
  60.8 0.6 multiply_reduce_fusion.2
  61.4 0.1 convert_reduce_fusion.1
  61.5 0.1 convolution_bitcast_fusion
  61.7 3.2 %fusion.1 = f32[512]{0:T(512)S(1)} fusion(f32[512,2048]{1,0:T(8,128)} %get-tuple-element.10, f32[512]{0:T(512)S(1)} %broadcast_multiply_fusion.2, f32[512]{0:T(512)S(1)} %get-tuple-element.5, f32[512]{0:T(512)S(1)} %copy-done.3), kind=kLoop, calls=%fused_computation.4 | loop fusion | flops 4193792 | bytes 4202496 | tf_op jit(solution)/shard_map/reduce_sum | solution.py:90
  64.8 20.6 %all-gather.3 = f32[4,1,512]{2,1,0:T(1,128)S(1)} all-gather(f32[1,1,512]{2,1,0:T(1,128)S(1)} %bitcast.30), channel_id=2, replica_groups=mesh['panel_0'=4,'panel_1'=4,'panel_2'=2,'samp'=8] {'panel_0'}, dimensions={0}, use_global_device_ids=true | all-gather | bytes 10240 | tf_op jit(solution)/shard_map/all_gather | solution.py:29
  85.4 10.9 %all-gather.4 = f32[4,1,512]{2,1,0:T(1,128)S(1)} all-gather(f32[1,1,512]{2,1,0:T(1,128)S(1)} %bitcast.33), channel_id=3, replica_groups=mesh['panel_0'=4,'panel_1'=4,'panel_2'=2,'samp'=8] {'panel_1'}, dimensions={0}, use_global_device_ids=true | all-gather | bytes 10240 | tf_op jit(solution)/shard_map/all_gather | solution.py:29
  96.4 7.0 %all-gather.5 = f32[2,1,512]{2,1,0:T(1,128)S(1)} all-gather(f32[1,1,512]{2,1,0:T(1,128)S(1)} %bitcast.34), channel_id=4, replica_groups=mesh['panel_0'=4,'panel_1'=4,'panel_2'=2,'samp'=8] {'panel_2'}, dimensions={0}, use_global_device_ids=true | all-gather | bytes 6144 | tf_op jit(solution)/shard_map/all_gather | solution.py:29
  103.5 1.7 %reduce_sum.129 = f32[512,32]{0,1:T(8,128)S(1)} reduce(f32[32,512,32]{1,2,0:T(8,128)} %all-to-all-done.2, f32[]{:T(128)} %constant.45.clone.1), dimensions={0}, to_apply=%region_5.0 | reduce | flops 507904 | bytes 2162692 | tf_op jit(solution)/shard_map/reduce_sum | solution.py:41
  105.2 1.0 multiply_reduce_fusion.1
  106.2 0.1 convolution_bitcast_fusion.1
  106.4 0.2 fusion.18
  106.6 0.8 concatenate.3
  107.3 0.6 broadcast_in_dim.8
  107.9 8.2 %all-to-all-start.3 = ((f32[8,1,369]{2,1,0:T(1,128)}), f32[8,1,369]{2,1,0:T(1,128)S(1)}, u32[]{:S(2)}, u32[]{:S(2)}) async-start(f32[8,1,369]{2,1,0:T(1,128)} %broadcast_in_dim.8), calls=%async_computation.3 | async-start | bytes 24576 | tf_op jit(solution)/shard_map/all_to_all | solution.py:14
  116.1 0.6 convert_element_type.34
  116.8 6.0 %all-to-all-done.3 = f32[8,1,369]{2,1,0:T(1,128)S(1)} async-done(((f32[8,1,369]{2,1,0:T(1,128)}), f32[8,1,369]{2,1,0:T(1,128)S(1)}, u32[]{:S(2)}, u32[]{:S(2)}) %all-to-all-start.3) | async-done | bytes 11840 | tf_op jit(solution)/shard_map/all_to_all | solution.py:14
  122.8 0.6 slice.25
  123.4 0.8 multiply_reduce_fusion.3
  125.6 0.7 fusion.17
  (22 shorter events, 0.6 us)
Async XLA Ops:
  0.6 13.5 %copy-start = (s32[512,1024]{1,0:T(8,128)S(1)}, s32[512,1024]{1,0:T(8,128)}, u32[]{:S(2)}) copy-start(s32[512,1024]{1,0:T(8,128)} %param.7) | copy-start | bytes 6291460
  5.5 16.2 %all-to-all-start = ((f32[32,1,1024]{2,1,0:T(1,128)}), f32[32,1,1024]{2,1,0:T(1,128)S(1)}, u32[]{:S(2)}, u32[]{:S(2)}) async-start(f32[32,1,1024]{2,1,0:T(1,128)} %broadcast_in_dim.6), calls=%async_computation | async-start | bytes 262144 | tf_op jit(solution)/shard_map/all_to_all | solution.py:14
  16.0 8.0 %copy-start.3 = (f32[512]{0:T(512)S(1)}, f32[512]{0:T(512)}, u32[]{:S(2)}) copy-start(f32[512]{0:T(512)} %param.9) | copy-start | bytes 6148
  54.3 6.5 %copy-start.1 = (f32[512]{0:T(512)S(1)}, f32[512]{0:T(512)}, u32[]{:S(2)}) copy-start(f32[512]{0:T(512)} %param.10) | copy-start | bytes 6148
  54.3 7.1 %copy-start.2 = (s32[512]{0:T(512)S(1)}, s32[512]{0:T(512)}, u32[]{:S(2)}) copy-start(s32[512]{0:T(512)} %param.11) | copy-start | bytes 6148
  54.3 49.1 %all-to-all-start.2 = ((f32[32,512,32]{1,2,0:T(8,128)}), f32[32,512,32]{1,2,0:T(8,128)}, u32[]{:S(2)}, u32[]{:S(2)}) async-start(f32[32,512,32]{1,2,0:T(8,128)} %bitcast.29), calls=%async_computation.2 | async-start | bytes 4194304 | tf_op jit(solution)/shard_map/all_to_all | solution.py:40
  107.9 14.8 %all-to-all-start.3 = ((f32[8,1,369]{2,1,0:T(1,128)}), f32[8,1,369]{2,1,0:T(1,128)S(1)}, u32[]{:S(2)}, u32[]{:S(2)}) async-start(f32[8,1,369]{2,1,0:T(1,128)} %broadcast_in_dim.8), calls=%async_computation.3 | async-start | bytes 24576 | tf_op jit(solution)/shard_map/all_to_all | solution.py:14
